TPU v7x, 32 devices: a whole 2x2x4 slice. The times are simulated.
32 devices in a mesh: gy: 4 (over z), gx: 8 (over y, x, core).
Axes of the slice: x: 2, y: 2, z: 4, core: 2. Of those that a mesh axis runs over, the one named last changes fastest.
Arguments:
- coefficients: float32 [9, 128, 256], P(None, 'gy', 'gx'), may hold values from -2.1 to 2.1
- vectors: float32 [128, 256, 2048], P('gy', 'gx'), may hold values from -6 to 6
Outputs:
- normal: float32 [25, 128, 256], P(None, 'gy', 'gx')
- image: float32 [128, 256, 2048], P('gy', 'gx')
All inputs are finite; a program needn't handle non-finite values.
Results may differ from a plain program's by a relative error of at most 0.00002.
Values sent between devices are 32-bit elements; how exact they have to be, the bound alone decides.
No kernel may reach another device: no remote copies, remote signals or barrier semaphores. Data moves between devices by JAX's collectives and lax.ppermute only.
A program may use at most 192 MiB of HBM per device.

v0:
```python
import jax
import jax.numpy as jnp
import numpy as np
from jax import lax
from jax.experimental import pallas as pl
from jax.experimental.pallas import tpu as pltpu
from jax.sharding import PartitionSpec as P


GROUP = 2


def inner_swap(block, axis):
    n = lax.axis_size(axis)
    return lax.ppermute(block, axis, [(i, i ^ 1) for i in range(n) if i ^ 1 < n])


def outer_swap(block, axis):
    n = lax.axis_size(axis)
    partner = {i: ((i + 1) ^ 1) - 1 for i in range(n)}
    return lax.ppermute(block, axis, [(i, p) for i, p in partner.items() if 0 <= p < n])


def masked_weights(coefficients):
    _, rows, cols = coefficients.shape
    total_rows = rows * lax.axis_size("gy")
    total_cols = cols * lax.axis_size("gx")
    k = jnp.arange(9, dtype=jnp.int32)[:, None, None]
    r = lax.axis_index("gy") * rows + jnp.arange(rows, dtype=jnp.int32)[None, :, None] + k // 3 - 1
    c = lax.axis_index("gx") * cols + jnp.arange(cols, dtype=jnp.int32)[None, None, :] + k % 3 - 1
    inside = (r >= 0) & (r < total_rows) & (c >= 0) & (c < total_cols)
    return jnp.where(inside, coefficients, 0.0)


def normal_terms(ext_ref, rows, cols):
    acc = {}
    for k in range(9):
        a, b = k // 3 - 1, k % 3 - 1
        cells = [ext_ref[m, 1 - a : 1 - a + rows, 1 - b : 1 - b + cols] for m in range(9)]
        for m in range(9):
            slot = (m // 3 - k // 3 + 2) * 5 + (m % 3 - k % 3 + 2)
            product = cells[k] * cells[m]
            acc[slot] = acc[slot] + product if slot in acc else product
    return acc


def split(x):
    hi = x.astype(jnp.bfloat16)
    lo = (x - hi.astype(jnp.float32)).astype(jnp.bfloat16)
    return hi, lo


def weights_kernel(rows, cols, pitch):
    m = GROUP * cols

    def body(ext_ref, t_ref, n_ref, w_ref, n2_ref):
        for slot, term in normal_terms(ext_ref, rows, cols).items():
            n_ref[slot] = term
            n2_ref[:, slot, :] = term
        n2_ref[:, 25:, :] = jnp.zeros((rows, n2_ref.shape[1] - 25, cols), jnp.float32)
        dims = (((0,), (0,)), ((), ()))
        for r in range(rows):
            g, ro = divmod(r, GROUP)
            n_hi, n_lo = split(n2_ref[r])
            band = lax.dot_general(n_hi, t_ref[...], dims, preferred_element_type=jnp.float32) + lax.dot_general(
                n_lo, t_ref[...], dims, preferred_element_type=jnp.float32
            )
            band = pltpu.roll(band, ro * pitch, 1, stride=1, stride_axis=0)
            hi, lo = split(band)
            w_ref[g, ro * cols : (ro + 1) * cols, :] = hi
            w_ref[g, m + ro * cols : m + (ro + 1) * cols, :] = lo

    return body


def image_kernel(rows, cols, pitch, depth):
    m = GROUP * cols

    def body(odd_ref, w_ref, x_ref, rin_ref, rout_ref, cin_ref, cout_ref, kin_ref, kout_ref, out_ref, hi_ref, lo_ref):
        lanes = x_ref.shape[1]
        odd_y = odd_ref[0] == 1
        odd_x = odd_ref[1] == 1

        pad = jnp.zeros((pitch - cols - 4, lanes), jnp.float32)

        def sides(near_ref, far_ref, q):
            near, far = near_ref[q], far_ref[q]
            return jnp.where(odd_x, near, far), jnp.where(odd_x, far, near)

        def wide_row(i):
            if i < 2:
                at = slice(i * cols, (i + 1) * cols)
                mid = jnp.where(odd_y, rin_ref[at, :], rout_ref[at, :])
                l, r = sides(kin_ref, kout_ref, i)
            elif i < rows + 2:
                q = i - 2
                mid = x_ref[q * cols : (q + 1) * cols, :]
                l, r = sides(cin_ref, cout_ref, q)
            else:
                q = i - rows - 2
                at = slice(q * cols, (q + 1) * cols)
                mid = jnp.where(odd_y, rout_ref[at, :], rin_ref[at, :])
                l, r = sides(kin_ref, kout_ref, q + 2)
            return [l, mid, r, pad]

        for i in range(0, rows + 4, 2):
            pair = jnp.concatenate(wide_row(i) + wide_row(i + 1), axis=0)
            hi, lo = split(pair)
            hi_ref[i * pitch : (i + 2) * pitch, :] = hi
            lo_ref[i * pitch : (i + 2) * pitch, :] = lo
        tail = hi_ref.shape[0] - (rows + 4) * pitch
        if tail:
            hi_ref[(rows + 4) * pitch :, :] = jnp.zeros((tail, lanes), jnp.bfloat16)
            lo_ref[(rows + 4) * pitch :, :] = jnp.zeros((tail, lanes), jnp.bfloat16)
        for g in range(rows // GROUP):
            at = g * GROUP * pitch
            first = jnp.dot(w_ref[g], hi_ref[at : at + depth, :], preferred_element_type=jnp.float32)
            second = jnp.dot(w_ref[g, :m, :], lo_ref[at : at + depth, :], preferred_element_type=jnp.float32)
            out_ref[g * m : (g + 1) * m, :] = first[:m] + (first[m:] + second)

    return body


def edges(cells, odd, dim, width):
    size = cells.shape[dim]
    last = lax.slice_in_dim(cells, size - width, size, axis=dim)
    first = lax.slice_in_dim(cells, 0, width, axis=dim)
    return jnp.where(odd, first, last), jnp.where(odd, last, first)


def swapped(pair, axis):
    outer = outer_swap(pair[1], axis)
    return inner_swap(pair[0], axis), outer


def per_device(coefficients, vectors):
    _, rows, cols = coefficients.shape
    nv = vectors.shape[2]
    odd_y = lax.axis_index("gy") % 2
    odd_x = lax.axis_index("gx") % 2
    oy, ox = odd_y == 1, odd_x == 1
    col_pair = edges(vectors, ox, 1, 2)
    cin, cout = swapped(col_pair, "gx")
    *col_pair, vectors = lax.optimization_barrier((*col_pair, vectors))
    row_last = lax.dynamic_slice_in_dim(vectors, jnp.where(oy, 0, rows - 2), 2, axis=0)
    row_first = lax.dynamic_slice_in_dim(vectors, jnp.where(oy, rows - 2, 0), 2, axis=0)
    row_last, row_first, coefficients = lax.optimization_barrier((row_last, row_first, coefficients))
    rin, rout = swapped((row_last, row_first), "gy")
    masked = masked_weights(coefficients)
    pair = edges(masked, oy, 1, 1)
    min_, mout = swapped(pair, "gy")
    ext = jnp.concatenate([jnp.where(oy, min_, mout), masked, jnp.where(oy, mout, min_)], axis=1)
    win, wout = swapped(edges(ext, ox, 2, 1), "gx")
    ext = jnp.concatenate([jnp.where(ox, win, wout), ext, jnp.where(ox, wout, win)], axis=2)
    pitch = -(-(cols + 4) // 8) * 8
    depth = -(-((GROUP + 4) * pitch) // 128) * 128
    spread = np.zeros((32, depth), np.float32)
    for s in range(25):
        spread[s, (s // 5) * pitch + s % 5] = 1.0
    lanes = min(nv, 256)
    wide_rows = (rows - GROUP) * pitch + depth
    wide_rows = -(-max(wide_rows, (rows + 4) * pitch) // 16) * 16
    m = GROUP * cols
    fixed = lambda *s: pl.BlockSpec(s, lambda j: (0,) * len(s))
    flat_block = lambda n: pl.BlockSpec((n, lanes), lambda j: (0, j))
    edge_block = lambda n: pl.BlockSpec((n, 2, lanes), lambda j: (0, 0, j))
    whole = pl.BlockSpec(memory_space=pltpu.VMEM)
    normal, banded = pl.pallas_call(
        weights_kernel(rows, cols, pitch),
        in_specs=[whole, whole],
        out_specs=[whole, whole],
        out_shape=[
            jax.ShapeDtypeStruct((25, rows, cols), jnp.float32),
            jax.ShapeDtypeStruct((rows // GROUP, 2 * m, depth), jnp.bfloat16),
        ],
        scratch_shapes=[pltpu.VMEM((rows, 32, cols), jnp.float32)],
        name="weights",
    )(ext, jnp.asarray(spread, jnp.bfloat16))
    rin, rout, banded = lax.optimization_barrier((rin, rout, banded))
    corner = []
    for vin, vout in zip(edges(rin, ox, 1, 2), edges(rout, ox, 1, 2)):
        corner.append(jnp.concatenate([jnp.where(oy, vin, vout), jnp.where(oy, vout, vin)], axis=0))
    kin, kout = swapped(corner, "gx")

    image = pl.pallas_call(
        image_kernel(rows, cols, pitch, depth),
        grid=(nv // lanes,),
        in_specs=[
            pl.BlockSpec(memory_space=pltpu.SMEM),
            fixed(rows // GROUP, 2 * m, depth),
            flat_block(rows * cols),
            flat_block(2 * cols),
            flat_block(2 * cols),
            edge_block(rows),
            edge_block(rows),
            edge_block(4),
            edge_block(4),
        ],
        out_specs=flat_block(rows * cols),
        out_shape=jax.ShapeDtypeStruct((rows * cols, nv), jnp.float32),
        scratch_shapes=[
            pltpu.VMEM((wide_rows, lanes), jnp.bfloat16),
            pltpu.VMEM((wide_rows, lanes), jnp.bfloat16),
        ],
        compiler_params=pltpu.CompilerParams(dimension_semantics=("arbitrary",)),
        name="image",
    )(
        jnp.stack([odd_y, odd_x]).astype(jnp.int32),
        banded,
        vectors.reshape(rows * cols, nv),
        rin.reshape(2 * cols, nv),
        rout.reshape(2 * cols, nv),
        cin,
        cout,
        kin,
        kout,
    )
    return normal, image.reshape(rows, cols, nv)


def solution(mesh):
    in_specs = (P(None, "gy", "gx"), P("gy", "gx", None))
    out_specs = (P(None, "gy", "gx"), P("gy", "gx", None))

    return jax.shard_map(per_device, mesh=mesh, in_specs=in_specs, out_specs=out_specs, check_vma=False)
```

profile of v0, /device:TPU:1, one launch (start us, length us, event | category | flops | bytes accessed | tf_op | source)
XLA Modules:
  0.0 50.7 jit_solution(8066962920468191597)
XLA Ops:
  0.7 2.8 %broadcast_select_fusion = (f32[32,2,2048]{2,1,0:T(2,128)S(1)}, f32[32,2,2048]{2,1,0:T(2,128)S(1)}) fusion(pred[]{:T(512)S(6)} %eq.11, f32[32,32,2048]{2,1,0:T(8,128)} %param.4), kind=kLoop, calls=%fused_computation | loop fusion | flops 262144 | bytes 2097153 | tf_op jit(solution)/shard_map/jit(_where)/select_n | solution.py:128
  3.5 2.3 %constant_dynamic-slice_fusion = (f32[2,32,2048]{2,1,0:T(8,128)}, f32[2,32,2048]{2,1,0:T(8,128)}) fusion(f32[32,32,2048]{2,1,0:T(8,128)} %param.4, s32[]{:T(128)S(6)} %select_n.145, s32[]{:T(128)S(6)} %select_n.144), kind=kLoop, calls=%fused_computation.38 | loop fusion | bytes 2097160 | tf_op jit(solution)/shard_map/dynamic_slice | solution.py:146
  5.8 0.1 fusion.4
  5.9 0.1 fusion.1
  6.0 1.0 %and_select_fusion = f32[9,32,32]{2,1,0:T(8,128)S(1)} fusion(f32[9,32,32]{2,1,0:T(8,128)} %param.3, pred[9,32]{1,0:T(8,128)(4,1)S(1)} %get-tuple-element.37, pred[9,32]{1,0:T(8,128)(4,1)S(1)} %get-tuple-element.36, pred[9,32]{1,0:T(8,128)(4,1)S(1)} %fusion.4), kind=kLoop, calls=%fused_computation.6 | loop fusion | flops 27648 | bytes 74592 | tf_op jit(solution)/shard_map/jit(_where)/select_n | solution.py:32
  7.0 2.2 %collective-permute-start = (f32[9,1,32]{2,1,0:T(1,128)S(1)}, f32[9,1,32]{2,1,0:T(1,128)S(1)}, u32[]{:S(2)}, u32[]{:S(2)}) collective-permute-start(f32[9,1,32]{2,1,0:T(1,128)S(1)} %get-tuple-element.32), channel_id=1, source_target_pairs={{0,8},{8,0},{16,24},{24,16},{1,9},{9,1},{17,25},{25,17},{2,10},{10... | collective-permute-start | bytes 3464 | tf_op jit(solution)/shard_map/ppermute | solution.py:15
  9.2 0.6 %collective-permute-start.1 = (f32[9,1,32]{2,1,0:T(1,128)S(1)}, f32[9,1,32]{2,1,0:T(1,128)S(1)}, u32[]{:S(2)}, u32[]{:S(2)}) collective-permute-start(f32[9,1,32]{2,1,0:T(1,128)S(1)} %get-tuple-element.33), channel_id=1, source_target_pairs={{8,16},{16,8},{9,17},{17,9},{10,18},{18,10},{11,19},{19,11},{12,20... | collective-permute-start | bytes 3464 | tf_op jit(solution)/shard_map/ppermute | solution.py:21
  9.9 3.9 %collective-permute-start.4 = (f32[2,32,2048]{2,1,0:T(8,128)}, f32[2,32,2048]{2,1,0:T(8,128)S(1)}, u32[]{:S(2)}, u32[]{:S(2)}) collective-permute-start(f32[2,32,2048]{2,1,0:T(8,128)} %get-tuple-element.14), channel_id=1, source_target_pairs={{0,8},{8,0},{16,24},{24,16},{1,9},{9,1},{17,25},{25,17},{2,10},{10... | collective-permute-start | bytes 1572872 | tf_op jit(solution)/shard_map/ppermute | solution.py:15
  13.8 0.7 %collective-permute-start.5 = (f32[2,32,2048]{2,1,0:T(8,128)}, f32[2,32,2048]{2,1,0:T(8,128)S(1)}, u32[]{:S(2)}, u32[]{:S(2)}) collective-permute-start(f32[2,32,2048]{2,1,0:T(8,128)} %get-tuple-element.15), channel_id=1, source_target_pairs={{8,16},{16,8},{9,17},{17,9},{10,18},{18,10},{11,19},{19,11},{12,20... | collective-permute-start | bytes 1572872 | tf_op jit(solution)/shard_map/ppermute | solution.py:21
  14.5 0.0 collective-permute-done
  14.5 0.0 collective-permute-done.1
  14.5 0.1 slice_select_fusion.1
  14.7 1.6 %collective-permute-start.2 = (f32[9,34,1]{2,1,0:T(8,128)S(1)}, f32[9,34,1]{2,1,0:T(8,128)S(1)}, u32[]{:S(2)}, u32[]{:S(2)}) collective-permute-start(f32[9,34,1]{2,1,0:T(8,128)S(1)} %get-tuple-element.30), channel_id=1, source_target_pairs={{0,1},{1,0},{2,3},{3,2},{4,5},{5,4},{6,7},{7,6},{8,9},{9,8},{10,11... | collective-permute-start | bytes 3680 | tf_op jit(solution)/shard_map/ppermute | solution.py:15
  16.2 3.0 %collective-permute-start.3 = (f32[9,34,1]{2,1,0:T(8,128)S(1)}, f32[9,34,1]{2,1,0:T(8,128)S(1)}, u32[]{:S(2)}, u32[]{:S(2)}) collective-permute-start(f32[9,34,1]{2,1,0:T(8,128)S(1)} %get-tuple-element.31), channel_id=1, source_target_pairs={{1,2},{2,1},{3,4},{4,3},{5,6},{6,5},{9,10},{10,9},{11,12},{12,11},... | collective-permute-start | bytes 3680 | tf_op jit(solution)/shard_map/ppermute | solution.py:21
  19.3 2.5 %collective-permute-start.7 = (f32[32,2,2048]{2,1,0:T(2,128)S(1)}, f32[32,2,2048]{2,1,0:T(2,128)S(1)}, u32[]{:S(2)}, u32[]{:S(2)}) collective-permute-start(f32[32,2,2048]{2,1,0:T(2,128)S(1)} %get-tuple-element.22), channel_id=1, source_target_pairs={{1,2},{2,1},{3,4},{4,3},{5,6},{6,5},{9,10},{10,9},{11,12},{12,11},... | collective-permute-start | bytes 1572872 | tf_op jit(solution)/shard_map/ppermute | solution.py:21
  21.8 0.0 collective-permute-done.2
  21.8 0.1 collective-permute-start.6
  21.9 3.2 %collective-permute-done.3 = f32[9,34,1]{2,1,0:T(8,128)S(1)} collective-permute-done((f32[9,34,1]{2,1,0:T(8,128)S(1)}, f32[9,34,1]{2,1,0:T(8,128)S(1)}, u32[]{:S(2)}, u32[]{:S(2)}) %collective-permute-start.3) | collective-permute-done | bytes 1256 | tf_op jit(solution)/shard_map/ppermute | solution.py:21
  25.1 0.9 %pad_maximum_fusion.1.ext_ref = f32[9,34,34]{2,1,0:T(8,128)} fusion(f32[9,34,1]{2,1,0:T(8,128)S(1)} %get-tuple-element.29, f32[9,1,32]{2,1,0:T(1,128)S(1)} %get-tuple-element.35, f32[9,32,32]{2,1,0:T(8,128)S(1)} %and_select_fusion, f32[9,1,32]{2,1,0:T(1,128)S(1)} %get-tuple-element.34, f32[9,34,1]{2,1,0:T(8,128)S(1)} %get-tuple-element.28), kind=kLoop, calls=%fused_computation.3 | loop fusion | flops 41616 | bytes 83232 | tf_op jit(solution)/shard_map/concatenate | solution.py:154
  26.0 3.5 %weights.1 = (f32[25,32,32]{2,1,0:T(8,128)}, bf16[16,128,256]{2,1,0:T(8,128)(2,1)}) custom-call(f32[9,34,34]{2,1,0:T(8,128)} %pad_maximum_fusion.1.ext_ref, bf16[32,256]{1,0:T(8,128)(2,1)} %constant.65.clone.t_ref), custom_call_target="tpu_custom_call" | custom-call | tf_op jit(solution)/shard_map/weights/pallas_call | solution.py:168
  29.5 0.0 collective-permute-done.4
  29.5 0.0 collective-permute-done.5
  29.5 0.1 broadcast_select_fusion.9
  29.6 0.1 collective-permute-start.8
  29.7 4.4 %collective-permute-start.9 = (f32[4,2,2048]{2,1,0:T(2,128)S(1)}, f32[4,2,2048]{2,1,0:T(2,128)S(1)}, u32[]{:S(2)}, u32[]{:S(2)}) collective-permute-start(f32[4,2,2048]{2,1,0:T(2,128)S(1)} %pad_maximum_fusion.3), channel_id=1, source_target_pairs={{1,2},{2,1},{3,4},{4,3},{5,6},{6,5},{9,10},{10,9},{11,12},{12,11},... | collective-permute-start | bytes 196616 | tf_op jit(solution)/shard_map/ppermute | solution.py:21
  34.1 0.7 %pad_add_fusion.odd_ref = s32[2]{0:T(128)} fusion(s32[1]{0:T(128)} %bitcast.1, s32[1]{0:T(128)} %bitcast), kind=kLoop, calls=%fused_computation.35 | loop fusion | flops 2 | bytes 16 | tf_op jit(solution)/shard_map/stack | solution.py:208
  34.8 1.2 %collective-permute-done.7.cout_ref = f32[32,2,2048]{2,1,0:T(2,128)S(1)} collective-permute-done((f32[32,2,2048]{2,1,0:T(2,128)S(1)}, f32[32,2,2048]{2,1,0:T(2,128)S(1)}, u32[]{:S(2)}, u32[]{:S(2)}) %collective-permute-start.7) | collective-permute-done | bytes 524320 | tf_op jit(solution)/shard_map/ppermute | solution.py:21
  36.0 0.0 collective-permute-done.6.cin_ref
  36.0 0.0 collective-permute-done.8.kin_ref
  36.0 1.4 %collective-permute-done.9.kout_ref = f32[4,2,2048]{2,1,0:T(2,128)S(1)} collective-permute-done((f32[4,2,2048]{2,1,0:T(2,128)S(1)}, f32[4,2,2048]{2,1,0:T(2,128)S(1)}, u32[]{:S(2)}, u32[]{:S(2)}) %collective-permute-start.9) | collective-permute-done | bytes 65568 | tf_op jit(solution)/shard_map/ppermute | solution.py:21
  37.4 0.6 %copy-done.5 = f32[4,2,2048]{2,1,0:T(2,128)} copy-done((f32[4,2,2048]{2,1,0:T(2,128)}, f32[4,2,2048]{2,1,0:T(2,128)S(1)}, u32[]{:S(2)}) %copy-start.5) | copy-done | bytes 65560
  38.0 12.7 %image.1 = f32[1024,2048]{1,0:T(8,128)} custom-call(s32[2]{0:T(128)} %pad_add_fusion.odd_ref, bf16[16,128,256]{2,1,0:T(8,128)(2,1)} %get-tuple-element.17.w_ref, f32[1024,2048]{1,0:T(8,128)} %bitcast.6, f32[64,2048]{1,0:T(8,128)} %bitcast.8, f32[64,2048]{1,0:T(8,128)} %bitcast.9, f32[32,2,2048]{2,1,0:T(2,128)} %copy-done.3, f32[32,2,2048]{2,1,0:T(2,128)} %copy-done.2, ...), custom_call_target="tpu_custom_call" | custom-call | tf_op jit(solution)/shard_map/image/pallas_call | solution.py:185
  (20 shorter events, 0.2 us)
Async XLA Ops:
  7.0 7.4 %collective-permute-start = (f32[9,1,32]{2,1,0:T(1,128)S(1)}, f32[9,1,32]{2,1,0:T(1,128)S(1)}, u32[]{:S(2)}, u32[]{:S(2)}) collective-permute-start(f32[9,1,32]{2,1,0:T(1,128)S(1)} %get-tuple-element.32), channel_id=1, source_target_pairs={{0,8},{8,0},{16,24},{24,16},{1,9},{9,1},{17,25},{25,17},{2,10},{10... | collective-permute-start | bytes 3464 | tf_op jit(solution)/shard_map/ppermute | solution.py:15
  9.2 5.3 %collective-permute-start.1 = (f32[9,1,32]{2,1,0:T(1,128)S(1)}, f32[9,1,32]{2,1,0:T(1,128)S(1)}, u32[]{:S(2)}, u32[]{:S(2)}) collective-permute-start(f32[9,1,32]{2,1,0:T(1,128)S(1)} %get-tuple-element.33), channel_id=1, source_target_pairs={{8,16},{16,8},{9,17},{17,9},{10,18},{18,10},{11,19},{19,11},{12,20... | collective-permute-start | bytes 3464 | tf_op jit(solution)/shard_map/ppermute | solution.py:21
  9.9 19.6 %collective-permute-start.4 = (f32[2,32,2048]{2,1,0:T(8,128)}, f32[2,32,2048]{2,1,0:T(8,128)S(1)}, u32[]{:S(2)}, u32[]{:S(2)}) collective-permute-start(f32[2,32,2048]{2,1,0:T(8,128)} %get-tuple-element.14), channel_id=1, source_target_pairs={{0,8},{8,0},{16,24},{24,16},{1,9},{9,1},{17,25},{25,17},{2,10},{10... | collective-permute-start | bytes 1572872 | tf_op jit(solution)/shard_map/ppermute | solution.py:15
  13.8 15.7 %collective-permute-start.5 = (f32[2,32,2048]{2,1,0:T(8,128)}, f32[2,32,2048]{2,1,0:T(8,128)S(1)}, u32[]{:S(2)}, u32[]{:S(2)}) collective-permute-start(f32[2,32,2048]{2,1,0:T(8,128)} %get-tuple-element.15), channel_id=1, source_target_pairs={{8,16},{16,8},{9,17},{17,9},{10,18},{18,10},{11,19},{19,11},{12,20... | collective-permute-start | bytes 1572872 | tf_op jit(solution)/shard_map/ppermute | solution.py:21
  14.7 7.2 %collective-permute-start.2 = (f32[9,34,1]{2,1,0:T(8,128)S(1)}, f32[9,34,1]{2,1,0:T(8,128)S(1)}, u32[]{:S(2)}, u32[]{:S(2)}) collective-permute-start(f32[9,34,1]{2,1,0:T(8,128)S(1)} %get-tuple-element.30), channel_id=1, source_target_pairs={{0,1},{1,0},{2,3},{3,2},{4,5},{5,4},{6,7},{7,6},{8,9},{9,8},{10,11... | collective-permute-start | bytes 3680 | tf_op jit(solution)/shard_map/ppermute | solution.py:15
  16.2 8.8 %collective-permute-start.3 = (f32[9,34,1]{2,1,0:T(8,128)S(1)}, f32[9,34,1]{2,1,0:T(8,128)S(1)}, u32[]{:S(2)}, u32[]{:S(2)}) collective-permute-start(f32[9,34,1]{2,1,0:T(8,128)S(1)} %get-tuple-element.31), channel_id=1, source_target_pairs={{1,2},{2,1},{3,4},{4,3},{5,6},{6,5},{9,10},{10,9},{11,12},{12,11},... | collective-permute-start | bytes 3680 | tf_op jit(solution)/shard_map/ppermute | solution.py:21
  19.3 16.7 %collective-permute-start.7 = (f32[32,2,2048]{2,1,0:T(2,128)S(1)}, f32[32,2,2048]{2,1,0:T(2,128)S(1)}, u32[]{:S(2)}, u32[]{:S(2)}) collective-permute-start(f32[32,2,2048]{2,1,0:T(2,128)S(1)} %get-tuple-element.22), channel_id=1, source_target_pairs={{1,2},{2,1},{3,4},{4,3},{5,6},{6,5},{9,10},{10,9},{11,12},{12,11},... | collective-permute-start | bytes 1572872 | tf_op jit(solution)/shard_map/ppermute | solution.py:21
  21.8 14.2 %collective-permute-start.6 = (f32[32,2,2048]{2,1,0:T(2,128)S(1)}, f32[32,2,2048]{2,1,0:T(2,128)S(1)}, u32[]{:S(2)}, u32[]{:S(2)}) collective-permute-start(f32[32,2,2048]{2,1,0:T(2,128)S(1)} %get-tuple-element.23), channel_id=1, source_target_pairs={{0,1},{1,0},{2,3},{3,2},{4,5},{5,4},{6,7},{7,6},{8,9},{9,8},{10,11... | collective-permute-start | bytes 1572872 | tf_op jit(solution)/shard_map/ppermute | solution.py:15
  29.5 7.9 %copy-start = (f32[2,32,2048]{2,1,0:T(8,128)}, f32[2,32,2048]{2,1,0:T(8,128)S(1)}, u32[]{:S(2)}) copy-start(f32[2,32,2048]{2,1,0:T(8,128)S(1)} %collective-permute-done.4) | copy-start | bytes 1572868
  29.5 7.9 %copy-start.1 = (f32[2,32,2048]{2,1,0:T(8,128)}, f32[2,32,2048]{2,1,0:T(8,128)S(1)}, u32[]{:S(2)}) copy-start(f32[2,32,2048]{2,1,0:T(8,128)S(1)} %collective-permute-done.5) | copy-start | bytes 1572868
  29.6 6.4 %collective-permute-start.8 = (f32[4,2,2048]{2,1,0:T(2,128)S(1)}, f32[4,2,2048]{2,1,0:T(2,128)S(1)}, u32[]{:S(2)}, u32[]{:S(2)}) collective-permute-start(f32[4,2,2048]{2,1,0:T(2,128)S(1)} %pad_maximum_fusion.2), channel_id=1, source_target_pairs={{0,1},{1,0},{2,3},{3,2},{4,5},{5,4},{6,7},{7,6},{8,9},{9,8},{10,11... | collective-permute-start | bytes 196616 | tf_op jit(solution)/shard_map/ppermute | solution.py:15
  29.7 7.7 %collective-permute-start.9 = (f32[4,2,2048]{2,1,0:T(2,128)S(1)}, f32[4,2,2048]{2,1,0:T(2,128)S(1)}, u32[]{:S(2)}, u32[]{:S(2)}) collective-permute-start(f32[4,2,2048]{2,1,0:T(2,128)S(1)} %pad_maximum_fusion.3), channel_id=1, source_target_pairs={{1,2},{2,1},{3,4},{4,3},{5,6},{6,5},{9,10},{10,9},{11,12},{12,11},... | collective-permute-start | bytes 196616 | tf_op jit(solution)/shard_map/ppermute | solution.py:21
  36.0 1.4 %copy-start.2 = (f32[32,2,2048]{2,1,0:T(2,128)}, f32[32,2,2048]{2,1,0:T(2,128)S(1)}, u32[]{:S(2)}) copy-start(f32[32,2,2048]{2,1,0:T(2,128)S(1)} %collective-permute-done.7.cout_ref) | copy-start | bytes 1572868
  36.0 1.4 %copy-start.3 = (f32[32,2,2048]{2,1,0:T(2,128)}, f32[32,2,2048]{2,1,0:T(2,128)S(1)}, u32[]{:S(2)}) copy-start(f32[32,2,2048]{2,1,0:T(2,128)S(1)} %collective-permute-done.6.cin_ref) | copy-start | bytes 1572868
  36.0 1.4 %copy-start.4 = (f32[4,2,2048]{2,1,0:T(2,128)}, f32[4,2,2048]{2,1,0:T(2,128)S(1)}, u32[]{:S(2)}) copy-start(f32[4,2,2048]{2,1,0:T(2,128)S(1)} %collective-permute-done.8.kin_ref) | copy-start | bytes 196612
  37.4 0.6 %copy-start.5 = (f32[4,2,2048]{2,1,0:T(2,128)}, f32[4,2,2048]{2,1,0:T(2,128)S(1)}, u32[]{:S(2)}) copy-start(f32[4,2,2048]{2,1,0:T(2,128)S(1)} %collective-permute-done.9.kout_ref) | copy-start | bytes 196612
where the time goes:
time: 51.2 us; the launch traced here: 50.7 us
  starting transfers between devices  19.1 us (37%)
  Pallas kernels  16.2 us (32%)
  other arithmetic  5.87 us (11%)
  waiting for transfers between devices  5.78 us (11%)
  local copies, waits for them, and re-layouts  2.89 us (6%)
  between operations  0.89 us (2%)
    pallas_call x1, Pallas kernels, per_device(): pl.pallas_call(image_kernel(rows, cols, pitch, depth), grid=(nv // lanes,...  12.7 us
    ppermute x5, starting transfers between devices, outer_swap(): lax.ppermute(block, axis, [(i, p) for i, p in partner.items() if 0 <= p <...  11.3 us
    ppermute x5, starting transfers between devices, inner_swap(): lax.ppermute(block, axis, [(i, i ^ 1) for i in range(n) if i ^ 1 < n])  7.81 us
    ppermute x5, waiting for transfers between devices, outer_swap(): lax.ppermute(block, axis, [(i, p) for i, p in partner.items() if 0 <= p <...  5.77 us
    pallas_call x1, Pallas kernels, per_device(): pl.pallas_call(weights_kernel(rows, cols, pitch), in_specs=[whole, whole]...  3.52 us
    select_n x3, other arithmetic, edges(): return (jnp.where(odd, first, last), jnp.where(odd, last, first))  2.96 us
    dynamic_slice x1, local copies, waits for them, and re-layouts, per_device(): lax.dynamic_slice_in_dim(vectors, jnp.where(oy, rows - 2, 0), 2, axis=0)  2.29 us
  transfers between devices with their start and end apart: 10, of which 3 were waited for; matrix products, arithmetic and copies ran while one was open for 4% of the time, Pallas kernels for 7%

commit v1 on v0

--- a/solution.py
+++ b/solution.py
@@ -8,6 +8,7 @@
 
 
 GROUP = 2
+STRIPS = 4
 
 
 def inner_swap(block, axis):
@@ -76,8 +77,11 @@
 def image_kernel(rows, cols, pitch, depth):
     m = GROUP * cols
 
-    def body(odd_ref, w_ref, x_ref, rin_ref, rout_ref, cin_ref, cout_ref, kin_ref, kout_ref, out_ref, hi_ref, lo_ref):
-        lanes = x_ref.shape[1]
+    def body(odd_ref, w_ref, *refs):
+        x_refs = refs[:STRIPS]
+        rin_ref, rout_ref, cin_ref, cout_ref, kin_ref, kout_ref, out_ref, hi_ref, lo_ref = refs[STRIPS:]
+        lanes = out_ref.shape[1]
+        strip = rows // STRIPS
         odd_y = odd_ref[0] == 1
         odd_x = odd_ref[1] == 1
 
@@ -94,7 +98,7 @@
                 l, r = sides(kin_ref, kout_ref, i)
             elif i < rows + 2:
                 q = i - 2
-                mid = x_ref[q * cols : (q + 1) * cols, :]
+                mid = x_refs[q // strip][q % strip * cols : (q % strip + 1) * cols, :]
                 l, r = sides(cin_ref, cout_ref, q)
             else:
                 q = i - rows - 2
@@ -139,19 +143,19 @@
     odd_y = lax.axis_index("gy") % 2
     odd_x = lax.axis_index("gx") % 2
     oy, ox = odd_y == 1, odd_x == 1
-    col_pair = edges(vectors, ox, 1, 2)
-    cin, cout = swapped(col_pair, "gx")
-    *col_pair, vectors = lax.optimization_barrier((*col_pair, vectors))
-    row_last = lax.dynamic_slice_in_dim(vectors, jnp.where(oy, 0, rows - 2), 2, axis=0)
-    row_first = lax.dynamic_slice_in_dim(vectors, jnp.where(oy, rows - 2, 0), 2, axis=0)
-    row_last, row_first, coefficients = lax.optimization_barrier((row_last, row_first, coefficients))
-    rin, rout = swapped((row_last, row_first), "gy")
     masked = masked_weights(coefficients)
     pair = edges(masked, oy, 1, 1)
     min_, mout = swapped(pair, "gy")
     ext = jnp.concatenate([jnp.where(oy, min_, mout), masked, jnp.where(oy, mout, min_)], axis=1)
-    win, wout = swapped(edges(ext, ox, 2, 1), "gx")
+    pair = edges(ext, ox, 2, 1)
+    win, wout = swapped(pair, "gx")
     ext = jnp.concatenate([jnp.where(ox, win, wout), ext, jnp.where(ox, wout, win)], axis=2)
+    col_pair = edges(vectors, ox, 1, 2)
+    cin, cout = swapped(col_pair, "gx")
+    row_last = lax.dynamic_slice_in_dim(vectors, jnp.where(oy, 0, rows - 2), 2, axis=0)
+    row_first = lax.dynamic_slice_in_dim(vectors, jnp.where(oy, rows - 2, 0), 2, axis=0)
+    rin, rout = swapped((row_last, row_first), "gy")
+
     pitch = -(-(cols + 4) // 8) * 8
     depth = -(-((GROUP + 4) * pitch) // 128) * 128
     spread = np.zeros((32, depth), np.float32)
@@ -188,7 +192,7 @@
         in_specs=[
             pl.BlockSpec(memory_space=pltpu.SMEM),
             fixed(rows // GROUP, 2 * m, depth),
-            flat_block(rows * cols),
+            *[pl.BlockSpec((rows // STRIPS * cols, lanes), lambda j, q=q: (q, j)) for q in range(STRIPS)],
             flat_block(2 * cols),
             flat_block(2 * cols),
             edge_block(rows),
@@ -207,7 +211,7 @@
     )(
         jnp.stack([odd_y, odd_x]).astype(jnp.int32),
         banded,
-        vectors.reshape(rows * cols, nv),
+        *[vectors.reshape(rows * cols, nv)] * STRIPS,
         rin.reshape(2 * cols, nv),
         rout.reshape(2 * cols, nv),
         cin,

time: 51.2 us -> 50.8 us (level)
  waiting for transfers between devices: 5.78 us -> 4.79 us
  starting transfers between devices: 19.1 us -> 20 us
    ppermute x5, starting transfers between devices: 7.81 us -> 9.2 us  [inner_swap(): lax.ppermute(block, axis, [(i, i ^ 1) for i in range(n) if i ^ 1 < n])]
    ppermute x5, waiting for transfers between devices: 5.77 us -> 4.78 us  [outer_swap(): lax.ppermute(block, axis, [(i, p) for i, p in partner.items() if 0 <= p <...]
  transfers between devices with their start and end apart: 10 -> 10, of which waited for: 3 -> 3; matrix products, arithmetic and copies ran while one was open for 4% -> 14% of each run, Pallas kernels for 7% -> 7%
where the time goes in v1:
time: 50.8 us; the launch traced here: 50.3 us
  starting transfers between devices  20 us (39%)
  Pallas kernels  16 us (31%)
  other arithmetic  5.84 us (11%)
  waiting for transfers between devices  4.79 us (9%)
  local copies, waits for them, and re-layouts  2.88 us (6%)
  between operations  0.86 us (2%)
    pallas_call x1, Pallas kernels, per_device(): pl.pallas_call(image_kernel(rows, cols, pitch, depth), grid=(nv // lanes,...  12.4 us
    ppermute x5, starting transfers between devices, outer_swap(): lax.ppermute(block, axis, [(i, p) for i, p in partner.items() if 0 <= p <...  10.8 us
    ppermute x5, starting transfers between devices, inner_swap(): lax.ppermute(block, axis, [(i, i ^ 1) for i in range(n) if i ^ 1 < n])  9.2 us
    ppermute x5, waiting for transfers between devices, outer_swap(): lax.ppermute(block, axis, [(i, p) for i, p in partner.items() if 0 <= p <...  4.78 us
    pallas_call x1, Pallas kernels, per_device(): pl.pallas_call(weights_kernel(rows, cols, pitch), in_specs=[whole, whole]...  3.52 us
    select_n x3, other arithmetic, edges(): return (jnp.where(odd, first, last), jnp.where(odd, last, first))  2.95 us
    dynamic_slice x1, local copies, waits for them, and re-layouts, per_device(): lax.dynamic_slice_in_dim(vectors, jnp.where(oy, rows - 2, 0), 2, axis=0)  2.28 us
    select_n x1, other arithmetic, masked_weights(): return jnp.where(inside, coefficients, 0.0)  1.02 us
  transfers between devices with their start and end apart: 10, of which 3 were waited for; matrix products, arithmetic and copies ran while one was open for 14% of the time, Pallas kernels for 7%

profile of v1, /device:TPU:1, one launch (start us, length us, event | category | flops | bytes accessed | tf_op | source)
XLA Modules:
  0.0 50.3 jit_solution(5454972923809237867)
XLA Ops:
  0.7 0.1 fusion.4
  0.8 0.1 fusion.1
  0.8 1.0 %and_select_fusion = f32[9,32,32]{2,1,0:T(8,128)S(1)} fusion(f32[9,32,32]{2,1,0:T(8,128)} %param.3, pred[9,32]{1,0:T(8,128)(4,1)S(1)} %get-tuple-element.29, pred[9,32]{1,0:T(8,128)(4,1)S(1)} %get-tuple-element.28, pred[9,32]{1,0:T(8,128)(4,1)S(1)} %fusion.4), kind=kLoop, calls=%fused_computation.6 | loop fusion | flops 27648 | bytes 74592 | tf_op jit(solution)/shard_map/jit(_where)/select_n | solution.py:33
  1.9 2.2 %collective-permute-start = (f32[9,1,32]{2,1,0:T(1,128)S(1)}, f32[9,1,32]{2,1,0:T(1,128)S(1)}, u32[]{:S(2)}, u32[]{:S(2)}) collective-permute-start(f32[9,1,32]{2,1,0:T(1,128)S(1)} %get-tuple-element.24), channel_id=1, source_target_pairs={{0,8},{8,0},{16,24},{24,16},{1,9},{9,1},{17,25},{25,17},{2,10},{10... | collective-permute-start | bytes 3464 | tf_op jit(solution)/shard_map/ppermute | solution.py:16
  4.1 0.6 %collective-permute-start.1 = (f32[9,1,32]{2,1,0:T(1,128)S(1)}, f32[9,1,32]{2,1,0:T(1,128)S(1)}, u32[]{:S(2)}, u32[]{:S(2)}) collective-permute-start(f32[9,1,32]{2,1,0:T(1,128)S(1)} %get-tuple-element.25), channel_id=1, source_target_pairs={{8,16},{16,8},{9,17},{17,9},{10,18},{18,10},{11,19},{19,11},{12,20... | collective-permute-start | bytes 3464 | tf_op jit(solution)/shard_map/ppermute | solution.py:22
  4.7 2.3 %constant_dynamic-slice_fusion = (f32[2,32,2048]{2,1,0:T(8,128)}, f32[2,32,2048]{2,1,0:T(8,128)}) fusion(f32[32,32,2048]{2,1,0:T(8,128)} %param.4, s32[]{:T(128)S(6)} %select_n.151, s32[]{:T(128)S(6)} %select_n.150), kind=kLoop, calls=%fused_computation.38 | loop fusion | bytes 2097160 | tf_op jit(solution)/shard_map/dynamic_slice | solution.py:156
  7.0 0.7 %collective-permute-start.5 = (f32[2,32,2048]{2,1,0:T(8,128)}, f32[2,32,2048]{2,1,0:T(8,128)S(1)}, u32[]{:S(2)}, u32[]{:S(2)}) collective-permute-start(f32[2,32,2048]{2,1,0:T(8,128)} %get-tuple-element.14), channel_id=1, source_target_pairs={{8,16},{16,8},{9,17},{17,9},{10,18},{18,10},{11,19},{19,11},{12,20... | collective-permute-start | bytes 1572872 | tf_op jit(solution)/shard_map/ppermute | solution.py:22
  7.7 5.1 %collective-permute-start.4 = (f32[2,32,2048]{2,1,0:T(8,128)}, f32[2,32,2048]{2,1,0:T(8,128)S(1)}, u32[]{:S(2)}, u32[]{:S(2)}) collective-permute-start(f32[2,32,2048]{2,1,0:T(8,128)} %get-tuple-element.15), channel_id=1, source_target_pairs={{0,8},{8,0},{16,24},{24,16},{1,9},{9,1},{17,25},{25,17},{2,10},{10... | collective-permute-start | bytes 1572872 | tf_op jit(solution)/shard_map/ppermute | solution.py:16
  12.8 0.0 collective-permute-done
  12.8 0.0 collective-permute-done.1
  12.9 0.1 slice_select_fusion.1
  13.0 1.6 %collective-permute-start.2 = (f32[9,34,1]{2,1,0:T(8,128)S(1)}, f32[9,34,1]{2,1,0:T(8,128)S(1)}, u32[]{:S(2)}, u32[]{:S(2)}) collective-permute-start(f32[9,34,1]{2,1,0:T(8,128)S(1)} %get-tuple-element.22), channel_id=1, source_target_pairs={{0,1},{1,0},{2,3},{3,2},{4,5},{5,4},{6,7},{7,6},{8,9},{9,8},{10,11... | collective-permute-start | bytes 3680 | tf_op jit(solution)/shard_map/ppermute | solution.py:16
  14.6 3.0 %collective-permute-start.3 = (f32[9,34,1]{2,1,0:T(8,128)S(1)}, f32[9,34,1]{2,1,0:T(8,128)S(1)}, u32[]{:S(2)}, u32[]{:S(2)}) collective-permute-start(f32[9,34,1]{2,1,0:T(8,128)S(1)} %get-tuple-element.23), channel_id=1, source_target_pairs={{1,2},{2,1},{3,4},{4,3},{5,6},{6,5},{9,10},{10,9},{11,12},{12,11},... | collective-permute-start | bytes 3680 | tf_op jit(solution)/shard_map/ppermute | solution.py:22
  17.6 2.8 %broadcast_select_fusion = (f32[32,2,2048]{2,1,0:T(2,128)S(1)}, f32[32,2,2048]{2,1,0:T(2,128)S(1)}) fusion(pred[]{:T(512)S(6)} %eq.11, f32[32,32,2048]{2,1,0:T(8,128)} %param.4), kind=kLoop, calls=%fused_computation | loop fusion | flops 262144 | bytes 2097153 | tf_op jit(solution)/shard_map/jit(_where)/select_n | solution.py:132
  20.5 2.5 %collective-permute-start.7 = (f32[32,2,2048]{2,1,0:T(2,128)S(1)}, f32[32,2,2048]{2,1,0:T(2,128)S(1)}, u32[]{:S(2)}, u32[]{:S(2)}) collective-permute-start(f32[32,2,2048]{2,1,0:T(2,128)S(1)} %get-tuple-element.12), channel_id=1, source_target_pairs={{1,2},{2,1},{3,4},{4,3},{5,6},{6,5},{9,10},{10,9},{11,12},{12,11},... | collective-permute-start | bytes 1572872 | tf_op jit(solution)/shard_map/ppermute | solution.py:22
  23.0 0.0 collective-permute-done.2
  23.0 0.1 collective-permute-start.6
  23.1 0.3 collective-permute-done.3
  23.4 0.9 %pad_maximum_fusion.1.ext_ref = f32[9,34,34]{2,1,0:T(8,128)} fusion(f32[9,34,1]{2,1,0:T(8,128)S(1)} %get-tuple-element.21, f32[9,1,32]{2,1,0:T(1,128)S(1)} %get-tuple-element.27, f32[9,32,32]{2,1,0:T(8,128)S(1)} %and_select_fusion, f32[9,1,32]{2,1,0:T(1,128)S(1)} %get-tuple-element.26, f32[9,34,1]{2,1,0:T(8,128)S(1)} %get-tuple-element.20), kind=kLoop, calls=%fused_computation.3 | loop fusion | flops 41616 | bytes 83232 | tf_op jit(solution)/shard_map/concatenate | solution.py:152
  24.3 3.5 %weights.1 = (f32[25,32,32]{2,1,0:T(8,128)}, bf16[16,128,256]{2,1,0:T(8,128)(2,1)}) custom-call(f32[9,34,34]{2,1,0:T(8,128)} %pad_maximum_fusion.1.ext_ref, bf16[32,256]{1,0:T(8,128)(2,1)} %constant.65.clone.t_ref), custom_call_target="tpu_custom_call" | custom-call | tf_op jit(solution)/shard_map/weights/pallas_call | solution.py:172
  27.8 0.0 collective-permute-done.5
  27.8 0.0 collective-permute-done.4
  27.8 0.1 broadcast_select_fusion.9
  27.9 0.2 collective-permute-start.8
  28.2 3.9 %collective-permute-start.9 = (f32[4,2,2048]{2,1,0:T(2,128)S(1)}, f32[4,2,2048]{2,1,0:T(2,128)S(1)}, u32[]{:S(2)}, u32[]{:S(2)}) collective-permute-start(f32[4,2,2048]{2,1,0:T(2,128)S(1)} %pad_maximum_fusion.3), channel_id=1, source_target_pairs={{1,2},{2,1},{3,4},{4,3},{5,6},{6,5},{9,10},{10,9},{11,12},{12,11},... | collective-permute-start | bytes 196616 | tf_op jit(solution)/shard_map/ppermute | solution.py:22
  32.2 0.7 %pad_add_fusion.odd_ref = s32[2]{0:T(128)} fusion(s32[1]{0:T(128)} %bitcast.1, s32[1]{0:T(128)} %bitcast), kind=kLoop, calls=%fused_computation.35 | loop fusion | flops 2 | bytes 16 | tf_op jit(solution)/shard_map/stack | solution.py:212
  32.8 3.1 %collective-permute-done.7.refs_7_ = f32[32,2,2048]{2,1,0:T(2,128)S(1)} collective-permute-done((f32[32,2,2048]{2,1,0:T(2,128)S(1)}, f32[32,2,2048]{2,1,0:T(2,128)S(1)}, u32[]{:S(2)}, u32[]{:S(2)}) %collective-permute-start.7) | collective-permute-done | bytes 524320 | tf_op jit(solution)/shard_map/ppermute | solution.py:22
  35.9 0.0 collective-permute-done.6.refs_6_
  35.9 0.0 collective-permute-done.8.refs_8_
  35.9 1.4 %collective-permute-done.9.refs_9_ = f32[4,2,2048]{2,1,0:T(2,128)S(1)} collective-permute-done((f32[4,2,2048]{2,1,0:T(2,128)S(1)}, f32[4,2,2048]{2,1,0:T(2,128)S(1)}, u32[]{:S(2)}, u32[]{:S(2)}) %collective-permute-start.9) | collective-permute-done | bytes 65568 | tf_op jit(solution)/shard_map/ppermute | solution.py:22
  37.3 0.6 %copy-done.5 = f32[4,2,2048]{2,1,0:T(2,128)} copy-done((f32[4,2,2048]{2,1,0:T(2,128)}, f32[4,2,2048]{2,1,0:T(2,128)S(1)}, u32[]{:S(2)}) %copy-start.5) | copy-done | bytes 65560
  37.9 12.4 %image.1 = f32[1024,2048]{1,0:T(8,128)} custom-call(s32[2]{0:T(128)} %pad_add_fusion.odd_ref, bf16[16,128,256]{2,1,0:T(8,128)(2,1)} %get-tuple-element.9.w_ref, f32[1024,2048]{1,0:T(8,128)} %bitcast.6, f32[1024,2048]{1,0:T(8,128)} %bitcast.7, f32[1024,2048]{1,0:T(8,128)} %bitcast.8, f32[1024,2048]{1,0:T(8,128)} %bitcast.9, f32[64,2048]{1,0:T(8,128)} %bitcast.12, ...), custom_call_target="tpu_custom_call" | custom-call | tf_op jit(solution)/shard_map/image/pallas_call | solution.py:189
  (20 shorter events, 0.2 us)
Async XLA Ops:
  1.9 10.9 %collective-permute-start = (f32[9,1,32]{2,1,0:T(1,128)S(1)}, f32[9,1,32]{2,1,0:T(1,128)S(1)}, u32[]{:S(2)}, u32[]{:S(2)}) collective-permute-start(f32[9,1,32]{2,1,0:T(1,128)S(1)} %get-tuple-element.24), channel_id=1, source_target_pairs={{0,8},{8,0},{16,24},{24,16},{1,9},{9,1},{17,25},{25,17},{2,10},{10... | collective-permute-start | bytes 3464 | tf_op jit(solution)/shard_map/ppermute | solution.py:16
  4.1 8.8 %collective-permute-start.1 = (f32[9,1,32]{2,1,0:T(1,128)S(1)}, f32[9,1,32]{2,1,0:T(1,128)S(1)}, u32[]{:S(2)}, u32[]{:S(2)}) collective-permute-start(f32[9,1,32]{2,1,0:T(1,128)S(1)} %get-tuple-element.25), channel_id=1, source_target_pairs={{8,16},{16,8},{9,17},{17,9},{10,18},{18,10},{11,19},{19,11},{12,20... | collective-permute-start | bytes 3464 | tf_op jit(solution)/shard_map/ppermute | solution.py:22
  7.0 20.8 %collective-permute-start.5 = (f32[2,32,2048]{2,1,0:T(8,128)}, f32[2,32,2048]{2,1,0:T(8,128)S(1)}, u32[]{:S(2)}, u32[]{:S(2)}) collective-permute-start(f32[2,32,2048]{2,1,0:T(8,128)} %get-tuple-element.14), channel_id=1, source_target_pairs={{8,16},{16,8},{9,17},{17,9},{10,18},{18,10},{11,19},{19,11},{12,20... | collective-permute-start | bytes 1572872 | tf_op jit(solution)/shard_map/ppermute | solution.py:22
  7.7 20.1 %collective-permute-start.4 = (f32[2,32,2048]{2,1,0:T(8,128)}, f32[2,32,2048]{2,1,0:T(8,128)S(1)}, u32[]{:S(2)}, u32[]{:S(2)}) collective-permute-start(f32[2,32,2048]{2,1,0:T(8,128)} %get-tuple-element.15), channel_id=1, source_target_pairs={{0,8},{8,0},{16,24},{24,16},{1,9},{9,1},{17,25},{25,17},{2,10},{10... | collective-permute-start | bytes 1572872 | tf_op jit(solution)/shard_map/ppermute | solution.py:16
  13.0 10.0 %collective-permute-start.2 = (f32[9,34,1]{2,1,0:T(8,128)S(1)}, f32[9,34,1]{2,1,0:T(8,128)S(1)}, u32[]{:S(2)}, u32[]{:S(2)}) collective-permute-start(f32[9,34,1]{2,1,0:T(8,128)S(1)} %get-tuple-element.22), channel_id=1, source_target_pairs={{0,1},{1,0},{2,3},{3,2},{4,5},{5,4},{6,7},{7,6},{8,9},{9,8},{10,11... | collective-permute-start | bytes 3680 | tf_op jit(solution)/shard_map/ppermute | solution.py:16
  14.6 8.8 %collective-permute-start.3 = (f32[9,34,1]{2,1,0:T(8,128)S(1)}, f32[9,34,1]{2,1,0:T(8,128)S(1)}, u32[]{:S(2)}, u32[]{:S(2)}) collective-permute-start(f32[9,34,1]{2,1,0:T(8,128)S(1)} %get-tuple-element.23), channel_id=1, source_target_pairs={{1,2},{2,1},{3,4},{4,3},{5,6},{6,5},{9,10},{10,9},{11,12},{12,11},... | collective-permute-start | bytes 3680 | tf_op jit(solution)/shard_map/ppermute | solution.py:22
  20.5 15.4 %collective-permute-start.7 = (f32[32,2,2048]{2,1,0:T(2,128)S(1)}, f32[32,2,2048]{2,1,0:T(2,128)S(1)}, u32[]{:S(2)}, u32[]{:S(2)}) collective-permute-start(f32[32,2,2048]{2,1,0:T(2,128)S(1)} %get-tuple-element.12), channel_id=1, source_target_pairs={{1,2},{2,1},{3,4},{4,3},{5,6},{6,5},{9,10},{10,9},{11,12},{12,11},... | collective-permute-start | bytes 1572872 | tf_op jit(solution)/shard_map/ppermute | solution.py:22
  23.0 12.9 %collective-permute-start.6 = (f32[32,2,2048]{2,1,0:T(2,128)S(1)}, f32[32,2,2048]{2,1,0:T(2,128)S(1)}, u32[]{:S(2)}, u32[]{:S(2)}) collective-permute-start(f32[32,2,2048]{2,1,0:T(2,128)S(1)} %get-tuple-element.13), channel_id=1, source_target_pairs={{0,1},{1,0},{2,3},{3,2},{4,5},{5,4},{6,7},{7,6},{8,9},{9,8},{10,11... | collective-permute-start | bytes 1572872 | tf_op jit(solution)/shard_map/ppermute | solution.py:16
  27.8 9.5 %copy-start = (f32[2,32,2048]{2,1,0:T(8,128)}, f32[2,32,2048]{2,1,0:T(8,128)S(1)}, u32[]{:S(2)}) copy-start(f32[2,32,2048]{2,1,0:T(8,128)S(1)} %collective-permute-done.5) | copy-start | bytes 1572868
  27.8 9.5 %copy-start.1 = (f32[2,32,2048]{2,1,0:T(8,128)}, f32[2,32,2048]{2,1,0:T(8,128)S(1)}, u32[]{:S(2)}) copy-start(f32[2,32,2048]{2,1,0:T(8,128)S(1)} %collective-permute-done.4) | copy-start | bytes 1572868
  27.9 7.9 %collective-permute-start.8 = (f32[4,2,2048]{2,1,0:T(2,128)S(1)}, f32[4,2,2048]{2,1,0:T(2,128)S(1)}, u32[]{:S(2)}, u32[]{:S(2)}) collective-permute-start(f32[4,2,2048]{2,1,0:T(2,128)S(1)} %pad_maximum_fusion.2), channel_id=1, source_target_pairs={{0,1},{1,0},{2,3},{3,2},{4,5},{5,4},{6,7},{7,6},{8,9},{9,8},{10,11... | collective-permute-start | bytes 196616 | tf_op jit(solution)/shard_map/ppermute | solution.py:16
  28.2 9.1 %collective-permute-start.9 = (f32[4,2,2048]{2,1,0:T(2,128)S(1)}, f32[4,2,2048]{2,1,0:T(2,128)S(1)}, u32[]{:S(2)}, u32[]{:S(2)}) collective-permute-start(f32[4,2,2048]{2,1,0:T(2,128)S(1)} %pad_maximum_fusion.3), channel_id=1, source_target_pairs={{1,2},{2,1},{3,4},{4,3},{5,6},{6,5},{9,10},{10,9},{11,12},{12,11},... | collective-permute-start | bytes 196616 | tf_op jit(solution)/shard_map/ppermute | solution.py:22
  35.9 1.4 %copy-start.2 = (f32[32,2,2048]{2,1,0:T(2,128)}, f32[32,2,2048]{2,1,0:T(2,128)S(1)}, u32[]{:S(2)}) copy-start(f32[32,2,2048]{2,1,0:T(2,128)S(1)} %collective-permute-done.7.refs_7_) | copy-start | bytes 1572868
  35.9 1.4 %copy-start.3 = (f32[32,2,2048]{2,1,0:T(2,128)}, f32[32,2,2048]{2,1,0:T(2,128)S(1)}, u32[]{:S(2)}) copy-start(f32[32,2,2048]{2,1,0:T(2,128)S(1)} %collective-permute-done.6.refs_6_) | copy-start | bytes 1572868
  35.9 1.4 %copy-start.4 = (f32[4,2,2048]{2,1,0:T(2,128)}, f32[4,2,2048]{2,1,0:T(2,128)S(1)}, u32[]{:S(2)}) copy-start(f32[4,2,2048]{2,1,0:T(2,128)S(1)} %collective-permute-done.8.refs_8_) | copy-start | bytes 196612
  37.3 0.6 %copy-start.5 = (f32[4,2,2048]{2,1,0:T(2,128)}, f32[4,2,2048]{2,1,0:T(2,128)S(1)}, u32[]{:S(2)}) copy-start(f32[4,2,2048]{2,1,0:T(2,128)S(1)} %collective-permute-done.9.refs_9_) | copy-start | bytes 196612
